TPU v7x, 128 devices: a whole 4x4x4 slice. The times are simulated.
128 devices in a mesh: group: 4 (over x_lo, core), shard: 32 (over z, y, x_hi).
Axes of the slice: x: 4 (x_hi: 2, x_lo: 2; x = x_hi * 2 + x_lo), y: 4, z: 4, core: 2. Of those that a mesh axis runs over, the one named last changes fastest.
Arguments:
- step_index: int32 [1], replicated, may hold values from 0 to 1023
- hidden: bfloat16 [4, 32768, 4608], P('group', 'shard'), may hold values from -600 to 600
- upstream: bfloat16 [4, 32768, 2304], P('group', 'shard'), may hold values from -40 to 40
- numerator: float32 [4, 4608, 2304], P('group', 'shard'), may hold values from -6 to 6
- push_weight: float32 [4], P('group'), may hold values from 0.5 to 2
Outputs:
- numerator_next: float32 [4, 4608, 2304], P('group', 'shard')
- weight_next: float32 [4], P('group')
- params: bfloat16 [4, 4608, 2304], P('group', 'shard')
All inputs are finite; a program needn't handle non-finite values.
Results may differ from a plain program's by a relative error of at most 0.009.
Values may be sent and summed in bfloat16 or wider, within the bound.
A program may use at most 128 MiB of HBM per device.

v0:
```python
from functools import partial

import jax
import jax.numpy as jnp
from jax import lax
from jax.sharding import PartitionSpec as P

learning_rate = 0.3
decay_steps = 256.0
clip_ceiling = 1.0
epsilon = 1e-06


def shortened(x):
    return jax.tree.map(lambda a: a.astype(jnp.bfloat16) if a.dtype == jnp.float32 else a, x)


def passed_along(x, axis, by):
    peers = lax.axis_size(axis)
    return lax.ppermute(x, axis, [(i, (i + by) % peers) for i in range(peers)])


def from_everyone(x, axis):
    copies = jnp.broadcast_to(x, (lax.axis_size(axis), *x.shape))
    return lax.all_to_all(copies, axis, split_axis=0, concat_axis=0, tiled=True)


def over_copies(x, axis):
    return from_everyone(x, axis).sum(axis=0)


def column_rows(own_hidden, own_upstream):
    return lax.dot_general(
        own_hidden, own_upstream, (((0,), (0,)), ((), ())), preferred_element_type=jnp.float32
    )


def shift_state(values, exponent):
    return jax.tree.map(
        lambda part, own: part.astype(own.dtype),
        passed_along(shortened(values), "group", 1 << exponent),
        values,
    )


def from_peer(shifter, values, offset_bit, level_count):
    branches = [partial(shifter, exponent=power_bit) for power_bit in range(level_count)]
    return lax.switch(offset_bit, branches, values)


def shards(step_index, hidden, upstream, numerator, push_weight):
    own_hidden = hidden[0]
    own_upstream = upstream[0]
    own_state = numerator[0]
    level_count = lax.axis_size("group").bit_length() - 1
    offset_bit = step_index[0] % level_count
    rate = learning_rate / jnp.sqrt(1.0 + step_index[0].astype(jnp.float32) / decay_steps)
    row_count = own_state.shape[0]
    entry_count = row_count * lax.axis_size("shard") * own_state.shape[1]
    gradient = lax.psum_scatter(
        column_rows(own_hidden, own_upstream).astype(jnp.bfloat16),
        "shard",
        scatter_dimension=0,
        tiled=True,
    ).astype(jnp.float32)
    square_sum = over_copies(jnp.sum(gradient * gradient), "shard")
    root_mean = jnp.sqrt(square_sum / entry_count + epsilon)
    factor = rate * jnp.minimum(1.0, clip_ceiling / root_mean)
    update = factor * gradient
    pushed = own_state - update
    peer_state, peer_weight = from_peer(shift_state, (pushed, push_weight), offset_bit, level_count)
    mixed_state = 0.5 * (pushed + peer_state)
    weight_next = 0.5 * (push_weight + peer_weight)
    new_params = (mixed_state / weight_next[0]).astype(jnp.bfloat16)
    return (mixed_state[None], weight_next, new_params[None])


def solution(mesh):
    placed = (
        P(),
        P("group", "shard", None),
        P("group", "shard", None),
        P("group", "shard", None),
        P("group"),
    )
    return jax.shard_map(
        shards,
        mesh=mesh,
        in_specs=placed,
        out_specs=(P("group", "shard", None), P("group"), P("group", "shard", None)),
        check_vma=False,
    )
```

profile of v0, /device:TPU:0, one launch (start us, length us, event | category | flops | bytes accessed | tf_op | source)
XLA Modules:
  0.0 368.5 jit_solution(2657570891398861547)
XLA Ops:
  7.2 0.0 reduce-scatter.2.cloned.1.call-start
  7.2 29.9 %convolution_convert_fusion = bf16[4608,2304]{1,0:T(8,128)(2,1)} fusion(bf16[1,1024,4608]{2,1,0:T(8,128)(2,1)} %param.8, bf16[1,1024,2304]{2,1,0:T(8,128)(2,1)} %param.9), kind=kOutput, calls=%fused_computation | convolution fusion | flops 21753888768 | bytes 35389440 | tf_op jit(solution)/shard_map/dot_general | solution.py:33
  37.2 0.0 copy-start
  37.2 0.0 reduce-scatter.2.cloned.1.call-update
  38.6 289.2 %reduce-scatter.2.cloned.1.call-done = bf16[144,2304]{1,0:T(8,128)(2,1)} async-done(((bf16[4608,2304]{1,0:T(8,128)(2,1)}), bf16[144,2304]{1,0:T(8,128)(2,1)}) %reduce-scatter.2.cloned.1.call-update) | async-done | bytes 663568 | tf_op jit(solution)/shard_map/reduce_scatter | solution.py:60
  327.8 2.0 fusion.2
  329.9 1.3 broadcast_in_dim.9
  331.1 4.6 %all-to-all-start = ((f32[32,1,1]{2,1,0:T(1,128)}), f32[32,1,1]{2,1,0:T(1,128)S(1)}, u32[]{:S(2)}, u32[]{:S(2)}) async-start(f32[32,1,1]{2,1,0:T(1,128)} %broadcast_in_dim.9), calls=%async_computation.1 | async-start | bytes 32768 | tf_op jit(solution)/shard_map/all_to_all | solution.py:25
  335.7 9.7 %all-to-all-done = f32[32,1,1]{2,1,0:T(1,128)S(1)} async-done(((f32[32,1,1]{2,1,0:T(1,128)}), f32[32,1,1]{2,1,0:T(1,128)S(1)}, u32[]{:S(2)}, u32[]{:S(2)}) %all-to-all-start) | async-done | bytes 160 | tf_op jit(solution)/shard_map/all_to_all | solution.py:25
  345.4 0.6 reduce_sum.19
  346.8 0.0 copy-done
  346.8 1.2 fusion.3
  348.0 11.1 %conditional.4 = (f32[144,2304]{1,0:T(8,128)S(1)}, f32[1]{0:T(128)}) conditional(s32[]{:T(128)} %clamp.3, (f32[144,2304]{1,0:T(8,128)S(1)}, f32[1]{0:T(128)}) %tuple.30, (f32[144,2304]{1,0:T(8,128)S(1)}, f32[1]{0:T(128)}) %tuple.30), branch_computations={%region_3.4_spmd, %region_4.5_spmd} | conditional | flops 663554 | bytes 6635636
  348.0 0.1 convert_element_type.36
  348.1 0.1 collective-permute-start
  348.8 2.6 collective-permute-start.1
  351.4 7.0 %collective-permute-done.1 = bf16[1]{0:T(256)(128)(2,1)} collective-permute-done((bf16[1]{0:T(256)(128)(2,1)}, bf16[1]{0:T(256)(128)(2,1)}, u32[]{:S(2)}, u32[]{:S(2)}) %collective-permute-start.1) | collective-permute-done | bytes 34 | tf_op jit(solution)/shard_map/cond/branch_0_fun/ppermute | solution.py:20
  359.0 0.0 collective-permute-done
  359.0 0.1 convert_element_type.54
  359.1 1.4 fusion.4
Async XLA Ops:
  7.2 320.7 %reduce-scatter.2.cloned.1.call-start = ((), (), s32[]{:S(2)}) async-start(), calls=%async_computation.2 | async-start | bytes 21897216 | tf_op jit(solution)/shard_map/reduce_scatter | solution.py:60
  37.2 309.6 %copy-start = (f32[1,144,2304]{2,1,0:T(8,128)S(1)}, f32[1,144,2304]{2,1,0:T(8,128)}, u32[]{:S(2)}) copy-start(f32[1,144,2304]{2,1,0:T(8,128)} %param.10) | copy-start | bytes 3981316
  331.1 14.3 %all-to-all-start = ((f32[32,1,1]{2,1,0:T(1,128)}), f32[32,1,1]{2,1,0:T(1,128)S(1)}, u32[]{:S(2)}, u32[]{:S(2)}) async-start(f32[32,1,1]{2,1,0:T(1,128)} %broadcast_in_dim.9), calls=%async_computation.1 | async-start | bytes 32768 | tf_op jit(solution)/shard_map/all_to_all | solution.py:25
  348.1 10.9 %collective-permute-start = (bf16[144,2304]{1,0:T(8,128)(2,1)S(1)}, bf16[144,2304]{1,0:T(8,128)(2,1)S(1)}, u32[]{:S(2)}, u32[]{:S(2)}) collective-permute-start(bf16[144,2304]{1,0:T(8,128)(2,1)S(1)} %convert_element_type.36), channel_id=1, source_target_pairs={{0,32},{32,64},{64,96},{96,0},{1,33},{33,65},{65,97},{97,1},{2,34}... | collective-permute-start | bytes 1990664 | tf_op jit(solution)/shard_map/cond/branch_0_fun/ppermute | solution.py:20
  348.8 9.5 %collective-permute-start.1 = (bf16[1]{0:T(256)(128)(2,1)}, bf16[1]{0:T(256)(128)(2,1)}, u32[]{:S(2)}, u32[]{:S(2)}) collective-permute-start(bf16[1]{0:T(256)(128)(2,1)} %convert_element_type.38), channel_id=1, source_target_pairs={{0,32},{32,64},{64,96},{96,0},{1,33},{33,65},{65,97},{97,1},{2,34}... | collective-permute-start | bytes 14 | tf_op jit(solution)/shard_map/cond/branch_0_fun/ppermute | solution.py:20
Sparse Core Ops, SparseCore 0:
  37.3 290.5 reduce-scatter.1
where the time goes:
time: 369 us
  waiting for transfers between devices  306 us (83%)
  matrix products  29.9 us (8%)
  between operations  17.3 us (5%)
  starting transfers between devices  7.27 us (2%)
  other arithmetic  5.49 us (1%)
    reduce_scatter x1, waiting for transfers between devices, shards(): lax.psum_scatter(column_rows(own_hidden, own_upstream).astype(jnp.bfloat1...  289 us
    dot_general x1, matrix products, column_rows(): lax.dot_general(own_hidden, own_upstream, (((0,), (0,)), ((), ())), prefe...  29.9 us
    all_to_all x1, waiting for transfers between devices, from_everyone(): return lax.all_to_all(copies, axis, split_axis=0, concat_axis=0, tiled=True)  9.69 us
  transfers between devices with their start and end apart: 4, of which 3 were waited for; matrix products, arithmetic and copies ran while one was open for 0% of the time, Pallas kernels for 0%

commit v1 on v0

v1 whole, which is shorter than its diff:
```python
import functools

import jax
import jax.numpy as jnp
from jax import lax
from jax.experimental import pallas as pl
from jax.experimental.pallas import tpu as pltpu
from jax.sharding import PartitionSpec as P

learning_rate = 0.3
decay_steps = 256.0
clip_ceiling = 1.0
epsilon = 1e-06

MESH = pl.DeviceIdType.MESH
RING = 4
LANES = 128
f32 = jnp.float32
bf16 = jnp.bfloat16


def kernel(
    entry_count,
    step_ref, weight_ref, hidden_hbm, upstream_hbm, numerator_hbm,
    gradient_out, peer_gradient_out, peer_numerator_out, coefficients_out,
    hidden, upstream, numerator, numerator_short, part, transit, final, across, last,
    gradient, gradient_short, squares, norms, meta,
    load_sem, out_sem, transit_send, transit_recv, final_send, final_recv,
    across_send, across_recv, last_send, last_recv, gossip_send, gossip_recv,
    state_send, state_recv, norm_send, norm_recv, meta_send, meta_recv,
):
    steps = part.shape[0]
    rows = part.shape[5]
    quarter = hidden.shape[1] // RING
    group = lax.axis_index("group")
    shard = lax.axis_index("shard")
    groups = lax.axis_size("group")
    shards = lax.axis_size("shard")
    z = shard // (2 * RING)
    y = (shard // 2) % RING
    xh = shard % 2

    def place(kind, first, second, half):
        zz, yy = (first, second) if kind == 0 else (second, first)
        return (group, zz * (2 * RING) + yy * 2 + half)

    def send(src, dst, send_sem, recv_sem, device):
        pltpu.make_async_remote_copy(
            src_ref=src, dst_ref=dst, send_sem=send_sem, recv_sem=recv_sem,
            device_id=device, device_id_type=MESH,
        ).start()

    def arrived(ref, sem):
        pltpu.make_async_copy(ref, ref, sem).wait()

    own = ((z, y), (y, z))

    def hidden_columns(i):
        block = (z + (2, 1, 3, 0)[i]) % RING if isinstance(i, int) else None
        return pl.ds(pl.multiple_of(block * quarter, LANES), quarter)

    wide = 2 * LANES
    loads = []
    loads.append(pltpu.make_async_copy(upstream_hbm.at[:, 0:wide], upstream.at[:, 0:wide], load_sem.at[4]))
    for i in range(RING):
        loads.append(pltpu.make_async_copy(
            hidden_hbm.at[:, hidden_columns(i)], hidden.at[:, hidden_columns(i)], load_sem.at[i]))
    loads.append(pltpu.make_async_copy(upstream_hbm.at[:, wide:], upstream.at[:, wide:], load_sem.at[5]))
    loads.append(pltpu.make_async_copy(numerator_hbm, numerator, load_sem.at[6]))
    for load in loads:
        load.start()

    barrier = pltpu.get_barrier_semaphore()
    partners = [(group, place(0, (z + k) % RING, y, xh)[1]) for k in range(1, RING)]
    partners += [(group, place(0, z, (y + k) % RING, xh)[1]) for k in range(1, RING)]
    partners += [(group, place(0, z, y, 1 - xh)[1])]
    partners += [((group + k) % groups, shard) for k in range(1, RING)]
    for device in partners:
        pl.semaphore_signal(barrier, inc=1, device_id=device, device_id_type=MESH)
    squares[...] = jnp.zeros_like(squares)
    loads[0].wait()

    def sum_of(*refs):
        total = refs[0][...].astype(f32)
        for ref in refs[1:]:
            total = total + ref[...].astype(f32)
        return total

    def open_step(t):
        columns = pl.ds(pl.multiple_of(t * wide, wide), wide)

        @pl.when(t == 1)
        def _():
            loads[5].wait()

        def block(i, carry):
            distance = jnp.where(i == 0, 2, jnp.where(i == 1, 1, jnp.where(i == 2, 3, 0)))
            to = (z + distance) % RING

            for j in range(RING):
                @pl.when((t == 0) & (i == j))
                def _(j=j):
                    loads[1 + j].wait()

            product = lax.dot_general(
                hidden[:, pl.ds(pl.multiple_of(to * quarter, LANES), quarter)],
                upstream[:, columns],
                (((0,), (0,)), ((), ())),
                preferred_element_type=f32,
            )
            for b in range(RING):
                for h in range(2):
                    at = (b * 2 + h) * rows
                    part[t, 0, to, h, b] = product[at:at + rows, :LANES].astype(bf16)
                    part[t, 1, b, h, to] = product[at:at + rows, LANES:].astype(bf16)

            @pl.when((t == 0) & (i == 0))
            def _():
                pl.semaphore_wait(barrier, len(partners))

            @pl.when(i == 0)
            def _():
                first_sends(t, 0)

            @pl.when(i == 1)
            def _():
                direct_send(t, 0, 1)

            @pl.when(i == 2)
            def _():
                direct_send(t, 0, 3)

            return carry

        lax.fori_loop(0, RING, block, 0)
        first_sends(t, 1)
        direct_send(t, 1, 1)
        direct_send(t, 1, 3)

    def first_sends(t, kind):
        a, b = own[kind]
        to = (a + 2) % RING
        for h, hop in ((0, 3), (1, 1)):
            send(part.at[t, kind, to, h], transit.at[t, kind, h], transit_send.at[t],
                 transit_recv.at[t, kind, h], place(kind, (a + hop) % RING, b, xh))

    def direct_send(t, kind, hop):
        a, b = own[kind]
        to = (a + hop) % RING
        h = 0 if hop == 1 else 1
        send(part.at[t, kind, to, h], final.at[t, kind, h], final_send.at[t],
             final_recv.at[t, kind], place(kind, to, b, xh))

    def relay_step(t):
        for kind in range(2):
            a, b = own[kind]
            for h, hop in ((0, 3), (1, 1)):
                to = (a + hop) % RING
                arrived(transit.at[t, kind, h], transit_recv.at[t, kind, h])
                part[t, kind, to, h] = sum_of(part.at[t, kind, to, h], transit.at[t, kind, h]).astype(bf16)
                send(part.at[t, kind, to, h], final.at[t, kind, 2 + h], final_send.at[t],
                     final_recv.at[t, kind], place(kind, to, b, xh))

    def across_step(t):
        for kind in range(2):
            a, b = own[kind]
            arrived(final.at[t, kind], final_recv.at[t, kind])
            for h in range(2):
                part[t, kind, a, h] = sum_of(
                    part.at[t, kind, a, h], final.at[t, kind, h], final.at[t, kind, 2 + h]).astype(bf16)
            send(part.at[t, kind, a, 1 - xh], across.at[t, kind], across_send.at[t],
                 across_recv.at[t, kind], place(kind, a, b, 1 - xh))

    def last_step(t):
        for kind in range(2):
            a, b = own[kind]
            arrived(across.at[t, kind], across_recv.at[t, kind])
            part[t, kind, a, xh] = sum_of(part.at[t, kind, a, xh], across.at[t, kind]).astype(bf16)
            for hop in (2, 1, 3):
                to = (b + hop) % RING
                send(part.at[t, kind, a, xh, to], last.at[t, kind, hop - 1], last_send.at[t],
                     last_recv.at[t, kind], place(kind, a, to, xh))

    def close_step(t):
        for kind in range(2):
            a, b = own[kind]
            arrived(last.at[t, kind], last_recv.at[t, kind])
            total = sum_of(part.at[t, kind, a, xh, b], last.at[t, kind, 0], last.at[t, kind, 1], last.at[t, kind, 2])
            at = slice(kind * LANES, (kind + 1) * LANES)
            gradient[t, :, at] = total
            gradient_short[t, :, at] = total.astype(bf16)
            squares[...] += jnp.sum((total * total).reshape(rows // 8, 8, LANES), axis=0)
        columns = pl.ds(pl.multiple_of(t * wide, wide), wide)
        for k in (1, 2):
            send(gradient_short.at[t], peer_gradient_out.at[k - 1, :, columns], gossip_send.at[t],
                 gossip_recv.at[k - 1], ((group + k) % groups, shard))
        pltpu.make_async_copy(gradient.at[t], gradient_out.at[:, columns], out_sem.at[t]).start()

    def turn(t, carry):
        @pl.when(t < steps)
        def _():
            open_step(t)

        @pl.when((t >= 1) & (t < steps + 1))
        def _():
            relay_step(t - 1)

        @pl.when(t == 0)
        def _():
            loads[6].wait()
            numerator_short[...] = numerator[...].astype(bf16)

        @pl.when(t == 1)
        def _():
            for k in (1, 2):
                send(numerator_short, peer_numerator_out.at[k - 1], state_send.at[k - 1],
                     state_recv.at[k - 1], ((group + k) % groups, shard))

        @pl.when((t >= 2) & (t < steps + 2))
        def _():
            across_step(t - 2)

        @pl.when((t >= 3) & (t < steps + 3))
        def _():
            last_step(t - 3)

        @pl.when(t >= 4)
        def _():
            close_step(t - 4)

        return carry

    lax.fori_loop(0, steps + 4, turn, 0)

    norms[0:1] = jnp.sum(squares[...], axis=0, keepdims=True)

    def tell(k, carry):
        send(norms.at[0:1], norms.at[pl.ds(k, 1)], norm_send.at[0], norm_recv.at[0], (group, (shard + k) % shards))
        return carry

    lax.fori_loop(1, shards, tell, 0)
    arrived(norms.at[1:shards], norm_recv.at[0])
    square_sum = jnp.sum(norms[...], keepdims=True)
    first_row = lax.broadcasted_iota(jnp.int32, (8, LANES), 0) == 0
    own_weight = jnp.full((8, LANES), weight_ref[0], f32)
    meta[0] = jnp.where(first_row, square_sum, own_weight)
    for k in (1, 2):
        send(meta.at[0], meta.at[k], meta_send.at[k - 1], meta_recv.at[k - 1], ((group + k) % groups, shard))

    arrived(norms.at[1:shards], norm_send.at[0])
    def drain(t, carry):
        arrived(transit.at[t], transit_send.at[t])
        arrived(final.at[t], final_send.at[t])
        arrived(across.at[t], across_send.at[t])
        arrived(last.at[t], last_send.at[t])
        pltpu.make_async_copy(gradient.at[t], gradient_out.at[:, 0:wide], out_sem.at[t]).wait()
        both = peer_gradient_out.at[:, :, 0:wide]
        arrived(both, gossip_send.at[t])
        return carry

    lax.fori_loop(0, steps, drain, 0)
    for k in range(2):
        arrived(peer_numerator_out.at[k], state_send.at[k])
        arrived(peer_numerator_out.at[k], state_recv.at[k])
        arrived(peer_gradient_out.at[k], gossip_recv.at[k])
        arrived(meta.at[k + 1], meta_send.at[k])
        arrived(meta.at[k + 1], meta_recv.at[k])

    step = step_ref[0]
    rate = learning_rate / jnp.sqrt(1.0 + jnp.full((8, LANES), step, jnp.int32).astype(f32) / decay_steps)
    far = jnp.full((8, LANES), step % 2, jnp.int32) == 1
    own_factor = rate * jnp.minimum(1.0, clip_ceiling / jnp.sqrt(square_sum / entry_count + epsilon))
    peer = jnp.where(far, meta[2], meta[1])
    peer_sum = jnp.broadcast_to(peer[0:1], (8, LANES))
    peer_factor = rate * jnp.minimum(1.0, clip_ceiling / jnp.sqrt(peer_sum / entry_count + epsilon))
    mixed_weight = 0.5 * (own_weight + jnp.broadcast_to(peer[1:2], (8, LANES)))
    coefficients_out[0] = own_factor
    coefficients_out[1] = peer_factor
    coefficients_out[2] = mixed_weight


def shards_step(mesh, step_index, hidden, upstream, numerator, push_weight):
    own_hidden, own_upstream, own_state = hidden[0], upstream[0], numerator[0]
    tokens, units = own_hidden.shape
    width = own_upstream.shape[1]
    rows = own_state.shape[0]
    shards = mesh.shape["shard"]
    steps = width // (2 * LANES)
    block = (RING, rows, LANES)
    anywhere = pl.BlockSpec(memory_space=pl.ANY)
    smem = pl.BlockSpec(memory_space=pltpu.SMEM)
    dma = pltpu.SemaphoreType.DMA
    gradient, peer_gradient, peer_numerator, coefficients = pl.pallas_call(
        functools.partial(kernel, float(rows * shards * width)),
        out_shape=(
            jax.ShapeDtypeStruct((rows, width), f32),
            jax.ShapeDtypeStruct((2, rows, width), bf16),
            jax.ShapeDtypeStruct((2, rows, width), bf16),
            jax.ShapeDtypeStruct((3, 8, LANES), f32),
        ),
        in_specs=[smem, smem, anywhere, anywhere, anywhere],
        out_specs=(anywhere, anywhere, anywhere, pl.BlockSpec(memory_space=pltpu.VMEM)),
        scratch_shapes=[
            pltpu.VMEM((tokens, units), bf16),
            pltpu.VMEM((tokens, width), bf16),
            pltpu.VMEM((rows, width), f32),
            pltpu.VMEM((rows, width), bf16),
            pltpu.VMEM((steps, 2, RING, 2) + block, bf16),
            pltpu.VMEM((steps, 2, 2) + block, bf16),
            pltpu.VMEM((steps, 2, 4) + block, bf16),
            pltpu.VMEM((steps, 2) + block, bf16),
            pltpu.VMEM((steps, 2, RING - 1, rows, LANES), bf16),
            pltpu.VMEM((steps, rows, 2 * LANES), f32),
            pltpu.VMEM((steps, rows, 2 * LANES), bf16),
            pltpu.VMEM((8, LANES), f32),
            pltpu.VMEM((shards, LANES), f32),
            pltpu.VMEM((3, 8, LANES), f32),
            dma((7,)), dma((steps,)),
            dma((steps,)), dma((steps, 2, 2)), dma((steps,)), dma((steps, 2)),
            dma((steps,)), dma((steps, 2)), dma((steps,)), dma((steps, 2)),
            dma((steps,)), dma((2,)), dma((2,)), dma((2,)), dma((1,)), dma((1,)), dma((2,)), dma((2,)),
        ],
        compiler_params=pltpu.CompilerParams(
            collective_id=0, has_side_effects=True, vmem_limit_bytes=67_043_328
        ),
        name="reduce_and_gossip",
    )(step_index, push_weight, own_hidden, own_upstream, own_state)
    own_factor, peer_factor, weight = (coefficients[i, 0, 0] for i in range(3))
    far = step_index[0] % 2 == 1
    peer_numerator = jnp.where(far, peer_numerator[1], peer_numerator[0]).astype(f32)
    peer_gradient = jnp.where(far, peer_gradient[1], peer_gradient[0]).astype(f32)
    pushed = own_state - own_factor * gradient
    mixed = 0.5 * (pushed + (peer_numerator - peer_factor * peer_gradient))
    return mixed[None], weight[None], (mixed / weight).astype(bf16)[None]


def solution(mesh):
    placed = (
        P(),
        P("group", "shard", None),
        P("group", "shard", None),
        P("group", "shard", None),
        P("group"),
    )
    return jax.shard_map(
        functools.partial(shards_step, mesh),
        mesh=mesh,
        in_specs=placed,
        out_specs=(P("group", "shard", None), P("group"), P("group", "shard", None)),
        check_vma=False,
    )
```

time: 369 us -> 143 us (0.39)
  waiting for transfers between devices: 306 us -> 0 us
  Pallas kernels: 0 us -> 133 us
  matrix products: 29.9 us -> 0 us
  between operations: 17.3 us -> 1.95 us
  starting transfers between devices: 7.27 us -> 0 us
    reduce_scatter x1 -> x0, waiting for transfers between devices: 289 us -> none  [shards(): lax.psum_scatter(column_rows(own_hidden, own_upstream).astype(jnp.bfloat1...]
    pallas_call x0 -> x1, Pallas kernels: none -> 133 us  [shards_step(): pl.pallas_call(functools.partial(kernel, float(rows * shards * width)), o...]
    dot_general x1 -> x0, matrix products: 29.9 us -> none  [column_rows(): lax.dot_general(own_hidden, own_upstream, (((0,), (0,)), ((), ())), prefe...]
    all_to_all x1 -> x0, waiting for transfers between devices: 9.69 us -> none  [from_everyone(): return lax.all_to_all(copies, axis, split_axis=0, concat_axis=0, tiled=True)]
    ppermute x2 -> x0, waiting for transfers between devices: 6.97 us -> none  [passed_along(): return lax.ppermute(x, axis, [(i, (i + by) % peers) for i in range(peers)])]
    broadcast_in_dim x1, other arithmetic: 1.44 us -> 6.28 us  [shards_step(): return (mixed[None], weight[None], (mixed / weight).astype(bf16)[None])]
    all_to_all x1 -> x0, starting transfers between devices: 4.58 us -> none  [from_everyone(): return lax.all_to_all(copies, axis, split_axis=0, concat_axis=0, tiled=True)]
  transfers between devices with their start and end apart: 4 -> 0, of which waited for: 3 -> 0; matrix products, arithmetic and copies ran while one was open for 0% -> 0% of each run, Pallas kernels for 0% -> 0%
where the time goes in v1:
time: 143 us; the launch traced here: 142 us
  Pallas kernels  133 us (93%)
  other arithmetic  6.28 us (4%)
  between operations  1.95 us (1%)
    pallas_call x1, Pallas kernels, shards_step(): pl.pallas_call(functools.partial(kernel, float(rows * shards * width)), o...  133 us
    broadcast_in_dim x1, other arithmetic, shards_step(): return (mixed[None], weight[None], (mixed / weight).astype(bf16)[None])  6.28 us

profile of v1, /device:TPU:0, one launch (start us, length us, event | category | flops | bytes accessed | tf_op | source)
XLA Modules:
  0.0 142.0 jit_solution(18411375468378678924)
XLA Ops:
  1.9 132.5 %reduce_and_gossip.1 = (f32[144,2304]{1,0:T(8,128)}, bf16[2,144,2304]{2,1,0:T(8,128)(2,1)}, bf16[2,144,2304]{2,1,0:T(8,128)(2,1)}, f32[3,8,128]{2,1,0:T(8,128)}) custom-call(s32[1]{0:T(128)} %copy.8.step_ref, f32[1]{0:T(128)S(6)} %copy.9.weight_ref, bf16[1024,4608]{1,0:T(8,128)(2,1)} %bitcast.21, bf16[1024,2304]{1,0:T(8,128)(2,1)} %bitcast.23, ...), custom_call_target="tpu_custom_call" | custom-call | tf_op jit(solution)/shard_map/reduce_and_gossip/pallas_call | solution.py:293
  134.5 1.3 fusion.3
  135.8 6.3 %fusion.1 = (bf16[1,144,2304]{2,1,0:T(8,128)(2,1)}, f32[144,2304]{1,0:T(8,128)}) fusion(f32[]{:T(128)} %bitcast.9, bf16[2,144,2304]{2,1,0:T(8,128)(2,1)} %get-tuple-element.10, f32[]{:T(128)} %bitcast.5, bf16[2,144,2304]{2,1,0:T(8,128)(2,1)} %get-tuple-element.9, pred[]{:T(512)S(6)} %eq.5, f32[144,2304]{1,0:T(8,128)} %get-tuple-element.8, f32[]{:T(128)} %bitcast.3, ...), kind=kLoop, calls=%fused_computation.3 | loop fusion | flops 3981312 | bytes 7299085 | tf_op jit(solution)/shard_map/broadcast_in_dim | solution.py:334
